TPU v7x, 512 devices: a whole 4x8x8 slice. The times are simulated.
512 devices in a mesh: tm: 32 (over y, z_lo), space: 16 (over x, z_hi, core).
Axes of the slice: x: 4, y: 8, z: 8 (z_hi: 2, z_lo: 4; z = z_hi * 4 + z_lo), core: 2. Of those that a mesh axis runs over, the one named last changes fastest.
Arguments:
- c_points: float32 [32, 256, 32, 128], P('tm', 'space'), may hold values from -15 to 15
- corrections: float32 [32, 256, 32, 128], P('tm', 'space'), may hold values from -3 to 3
- conductivity: float32 [256, 32, 128], P('space'), may hold values from 0.2 to 5
- forcing: float32 [256, 32, 128], P('space'), may hold values from -6 to 6
Outputs:
- f_states: float32 [32, 2, 256, 32, 128], P('tm', None, 'space')
All inputs are finite; a program needn't handle non-finite values.
Results may differ from a plain program's by a relative error of at most 0.0002.
Values sent between devices are 32-bit elements; how exact they have to be, the bound alone decides.
A program may use at most 64 MiB of HBM per device.

v0:
```python
import jax
import jax.numpy as jnp
from jax import lax
from jax.sharding import PartitionSpec as P

ITERS = 6
STEPS = 2


step_rate = 4.0
source_weight = 0.25


def copy_for_each(array, axis):
    devices = lax.axis_size(axis)
    return lax.all_to_all(
        jnp.broadcast_to(array[None], (devices, *array.shape)), axis, 0, 0, tiled=True
    )


def over_copies(array, axis):
    return copy_for_each(array, axis).sum(axis=0)


def packed_total(arrays, axis):
    ends = [0]
    for a in arrays:
        ends.append(ends[-1] + a.size)
    subtotal = over_copies(jnp.concatenate([a.ravel() for a in arrays]), axis)
    return tuple((subtotal[b:e].reshape(a.shape) for a, b, e in zip(arrays, ends, ends[1:])))


def extended(cells, sides, width):
    for axis, dim in sides:
        count = lax.axis_size(axis)
        ends = count - 1
        head = lax.slice_in_dim(cells, 0, width, axis=dim)
        tail = lax.slice_in_dim(cells, cells.shape[dim] - width, cells.shape[dim], axis=dim)
        cells = jnp.concatenate(
            [
                lax.ppermute(tail, axis, [(i, (i + 1) % count) for i in range(ends)]),
                cells,
                lax.ppermute(head, axis, [((i + 1) % count, i) for i in range(ends)]),
            ],
            axis=dim,
        )
    return cells


def from_behind(array, axis, by):
    devices = lax.axis_size(axis)
    pairs = [(i, i + by) for i in range(devices) if 0 <= i + by < devices]
    return lax.ppermute(array, axis, pairs)


def neighbours(padded):
    return (
        padded[2:, 1:-1, 1:-1],
        padded[:-2, 1:-1, 1:-1],
        padded[1:-1, 2:, 1:-1],
        padded[1:-1, :-2, 1:-1],
        padded[1:-1, 1:-1, 2:],
        padded[1:-1, 1:-1, :-2],
    )


def faces_of(padded_conductivity):
    centre = padded_conductivity[1:-1, 1:-1, 1:-1]
    return tuple((0.5 * (centre + beside) for beside in neighbours(padded_conductivity)))


def apply_operator(grid_field, padded, face_weights):
    flux_sum = jnp.zeros_like(grid_field)
    for face_weight, beside in zip(face_weights, neighbours(padded)):
        flux_sum = flux_sum + face_weight * (grid_field - beside)
    return grid_field + step_rate * flux_sum


def pair_sums(residual, applied):
    return packed_total((jnp.sum(residual * residual), jnp.sum(residual * applied)), "space")


def body(c_points, corrections, conductivity, forcing):
    rim_conductivity = extended(conductivity, (("space", 0),), 1)
    face_weights = faces_of(jnp.pad(rim_conductivity, ((0, 0), (1, 1), (1, 1))))

    def operate(grid_field):
        with_planes = extended(grid_field, (("space", 0),), 1)
        padded = jnp.pad(with_planes, ((0, 0), (1, 1), (1, 1)))
        return apply_operator(grid_field, padded, face_weights)

    own_point = c_points[0]
    own_fix = corrections[0]
    prior_fix = from_behind(own_fix, "tm", 1)
    current = own_point + prior_fix
    current_image = operate(current)
    sections = []
    for section in range(STEPS):
        right_side = current + source_weight * forcing
        if section > 0:
            current_image = operate(current)
        residual = right_side - current_image
        solution = current
        applied = operate(residual)
        norm_now, product = pair_sums(residual, applied)
        step_length = norm_now / product
        direction = residual
        along_dir = applied
        for sweep in range(ITERS):
            solution = solution + step_length * direction
            if sweep + 1 < ITERS:
                residual = residual - step_length * along_dir
                applied = operate(residual)
                norm_next, product = pair_sums(residual, applied)
                beta_ratio = norm_next / norm_now
                step_length = norm_next / (product - beta_ratio * norm_next / step_length)
                direction = residual + beta_ratio * direction
                along_dir = applied + beta_ratio * along_dir
                norm_now = norm_next
        sections.append(solution)
        current = solution
    return jnp.stack(sections)[None]


def solution(mesh):
    in_specs = (
        P("tm", "space", None, None),
        P("tm", "space", None, None),
        P("space", None, None),
        P("space", None, None),
    )
    out_specs = P("tm", None, "space", None, None)
    return jax.shard_map(body, mesh=mesh, in_specs=in_specs, out_specs=out_specs, check_vma=False)
```

profile of v0, /device:TPU:1, one launch (start us, length us, event | category | flops | bytes accessed | tf_op | source)
XLA Modules:
  0.0 497.6 jit_solution(16655384349083562095)
XLA Ops:
  0.0 4.8 collective-permute-start
  5.6 10.6 %collective-permute-start.3 = (f32[1,32,128]{2,1,0:T(8,128)S(1)}, f32[1,32,128]{2,1,0:T(8,128)S(1)}, u32[]{:S(2)}, u32[]{:S(2)}) collective-permute-start(f32[1,32,128]{2,1,0:T(8,128)S(1)} %get-tuple-element.74), channel_id=1, source_target_pairs={{0,1},{1,2},{2,3},{3,4},{4,5},{5,6},{6,7},{7,8},{8,9},{9,10},{10,1... | collective-permute-start | bytes 49160 | tf_op jit(solution)/shard_map/ppermute | solution.py:41
  16.2 2.1 collective-permute-start.1
  19.2 7.5 %collective-permute-start.4 = (f32[1,32,128]{2,1,0:T(8,128)S(1)}, f32[1,32,128]{2,1,0:T(8,128)S(1)}, u32[]{:S(2)}, u32[]{:S(2)}) collective-permute-start(f32[1,32,128]{2,1,0:T(8,128)S(1)} %get-tuple-element.76), channel_id=1, source_target_pairs={{0,1},{1,2},{2,3},{3,4},{4,5},{5,6},{6,7},{7,8},{8,9},{9,10},{10,1... | collective-permute-start | bytes 49160 | tf_op jit(solution)/shard_map/ppermute | solution.py:41
  26.8 1.9 collective-permute-start.2
  29.0 6.7 %collective-permute-done.2 = f32[1,32,128]{2,1,0:T(8,128)S(1)} collective-permute-done((f32[1,32,128]{2,1,0:T(8,128)S(1)}, f32[1,32,128]{2,1,0:T(8,128)S(1)}, u32[]{:S(2)}, u32[]{:S(2)}) %collective-permute-start.2) | collective-permute-done | bytes 16416 | tf_op jit(solution)/shard_map/ppermute | solution.py:43
  36.6 1.9 collective-permute-start.6
  38.6 2.4 collective-permute-start.5
  41.0 6.5 %collective-permute-done.5 = f32[1,32,128]{2,1,0:T(8,128)S(1)} collective-permute-done((f32[1,32,128]{2,1,0:T(8,128)S(1)}, f32[1,32,128]{2,1,0:T(8,128)S(1)}, u32[]{:S(2)}, u32[]{:S(2)}) %collective-permute-start.5) | collective-permute-done | bytes 16416 | tf_op jit(solution)/shard_map/ppermute | solution.py:43
  48.8 1.4 pad_maximum_fusion.30
  50.2 15.2 %all_to_all.72 = f32[16,1,2]{2,1,0:T(1,128)S(1)} all-to-all(f32[16,1,2]{2,1,0:T(1,128)S(1)} %broadcast_in_dim.26), channel_id=1, replica_groups=mesh['tm'=32,'space'=16] {'space'}, dimensions={0} | all-to-all | bytes 256 | tf_op jit(solution)/shard_map/all_to_all | solution.py:16
  67.4 2.8 collective-permute-start.8
  70.1 1.9 collective-permute-start.7
  72.1 7.0 %collective-permute-done.7 = f32[1,32,128]{2,1,0:T(8,128)S(1)} collective-permute-done((f32[1,32,128]{2,1,0:T(8,128)S(1)}, f32[1,32,128]{2,1,0:T(8,128)S(1)}, u32[]{:S(2)}, u32[]{:S(2)}) %collective-permute-start.7) | collective-permute-done | bytes 16416 | tf_op jit(solution)/shard_map/ppermute | solution.py:43
  81.8 18.5 %all_to_all.73 = f32[16,1,2]{2,1,0:T(1,128)S(1)} all-to-all(f32[16,1,2]{2,1,0:T(1,128)S(1)} %broadcast_in_dim.27), channel_id=1, replica_groups=mesh['tm'=32,'space'=16] {'space'}, dimensions={0} | all-to-all | bytes 256 | tf_op jit(solution)/shard_map/all_to_all | solution.py:16
  105.5 2.8 collective-permute-start.10
  108.3 1.9 collective-permute-start.9
  110.3 7.0 %collective-permute-done.9 = f32[1,32,128]{2,1,0:T(8,128)S(1)} collective-permute-done((f32[1,32,128]{2,1,0:T(8,128)S(1)}, f32[1,32,128]{2,1,0:T(8,128)S(1)}, u32[]{:S(2)}, u32[]{:S(2)}) %collective-permute-start.9) | collective-permute-done | bytes 16416 | tf_op jit(solution)/shard_map/ppermute | solution.py:43
  117.5 1.7 multiply_reduce_fusion.17
  120.5 18.4 %all_to_all.74 = f32[16,1,2]{2,1,0:T(1,128)S(1)} all-to-all(f32[16,1,2]{2,1,0:T(1,128)S(1)} %broadcast_in_dim.28), channel_id=1, replica_groups=mesh['tm'=32,'space'=16] {'space'}, dimensions={0} | all-to-all | bytes 256 | tf_op jit(solution)/shard_map/all_to_all | solution.py:16
  144.5 2.8 collective-permute-start.12
  147.3 1.9 collective-permute-start.11
  149.2 7.0 %collective-permute-done.11 = f32[1,32,128]{2,1,0:T(8,128)S(1)} collective-permute-done((f32[1,32,128]{2,1,0:T(8,128)S(1)}, f32[1,32,128]{2,1,0:T(8,128)S(1)}, u32[]{:S(2)}, u32[]{:S(2)}) %collective-permute-start.11) | collective-permute-done | bytes 16416 | tf_op jit(solution)/shard_map/ppermute | solution.py:43
  158.9 18.4 %all_to_all.75 = f32[16,1,2]{2,1,0:T(1,128)S(1)} all-to-all(f32[16,1,2]{2,1,0:T(1,128)S(1)} %broadcast_in_dim.29), channel_id=1, replica_groups=mesh['tm'=32,'space'=16] {'space'}, dimensions={0} | all-to-all | bytes 256 | tf_op jit(solution)/shard_map/all_to_all | solution.py:16
  181.8 2.8 collective-permute-start.14
  184.6 1.9 collective-permute-start.13
  186.5 7.0 %collective-permute-done.13 = f32[1,32,128]{2,1,0:T(8,128)S(1)} collective-permute-done((f32[1,32,128]{2,1,0:T(8,128)S(1)}, f32[1,32,128]{2,1,0:T(8,128)S(1)}, u32[]{:S(2)}, u32[]{:S(2)}) %collective-permute-start.13) | collective-permute-done | bytes 16416 | tf_op jit(solution)/shard_map/ppermute | solution.py:43
  193.8 1.7 multiply_reduce_fusion.13
  196.8 18.4 %all_to_all.76 = f32[16,1,2]{2,1,0:T(1,128)S(1)} all-to-all(f32[16,1,2]{2,1,0:T(1,128)S(1)} %broadcast_in_dim.30), channel_id=1, replica_groups=mesh['tm'=32,'space'=16] {'space'}, dimensions={0} | all-to-all | bytes 256 | tf_op jit(solution)/shard_map/all_to_all | solution.py:16
  220.7 2.8 collective-permute-start.16
  223.4 1.9 collective-permute-start.15
  225.4 7.0 %collective-permute-done.15 = f32[1,32,128]{2,1,0:T(8,128)S(1)} collective-permute-done((f32[1,32,128]{2,1,0:T(8,128)S(1)}, f32[1,32,128]{2,1,0:T(8,128)S(1)}, u32[]{:S(2)}, u32[]{:S(2)}) %collective-permute-start.15) | collective-permute-done | bytes 16416 | tf_op jit(solution)/shard_map/ppermute | solution.py:43
  233.7 1.4 pad_maximum_fusion.35
  235.1 18.4 %all_to_all.77 = f32[16,1,2]{2,1,0:T(1,128)S(1)} all-to-all(f32[16,1,2]{2,1,0:T(1,128)S(1)} %broadcast_in_dim.31), channel_id=1, replica_groups=mesh['tm'=32,'space'=16] {'space'}, dimensions={0} | all-to-all | bytes 256 | tf_op jit(solution)/shard_map/all_to_all | solution.py:16
  258.4 2.8 collective-permute-start.18
  261.2 2.1 collective-permute-start.17
  263.3 7.0 %collective-permute-done.17 = f32[1,32,128]{2,1,0:T(8,128)S(1)} collective-permute-done((f32[1,32,128]{2,1,0:T(8,128)S(1)}, f32[1,32,128]{2,1,0:T(8,128)S(1)}, u32[]{:S(2)}, u32[]{:S(2)}) %collective-permute-start.17) | collective-permute-done | bytes 16416 | tf_op jit(solution)/shard_map/ppermute | solution.py:43
  271.0 1.9 collective-permute-start.20
  272.9 2.4 collective-permute-start.19
  275.3 7.3 %collective-permute-done.19 = f32[1,32,128]{2,1,0:T(8,128)S(1)} collective-permute-done((f32[1,32,128]{2,1,0:T(8,128)S(1)}, f32[1,32,128]{2,1,0:T(8,128)S(1)}, u32[]{:S(2)}, u32[]{:S(2)}) %collective-permute-start.19) | collective-permute-done | bytes 16416 | tf_op jit(solution)/shard_map/ppermute | solution.py:43
  285.3 18.6 %all_to_all.78 = f32[16,1,2]{2,1,0:T(1,128)S(1)} all-to-all(f32[16,1,2]{2,1,0:T(1,128)S(1)} %broadcast_in_dim.32), channel_id=1, replica_groups=mesh['tm'=32,'space'=16] {'space'}, dimensions={0} | all-to-all | bytes 256 | tf_op jit(solution)/shard_map/all_to_all | solution.py:16
  305.8 2.8 collective-permute-start.22
  308.6 1.9 collective-permute-start.21
  310.5 7.0 %collective-permute-done.21 = f32[1,32,128]{2,1,0:T(8,128)S(1)} collective-permute-done((f32[1,32,128]{2,1,0:T(8,128)S(1)}, f32[1,32,128]{2,1,0:T(8,128)S(1)}, u32[]{:S(2)}, u32[]{:S(2)}) %collective-permute-start.21) | collective-permute-done | bytes 16416 | tf_op jit(solution)/shard_map/ppermute | solution.py:43
  320.3 18.4 %all_to_all.79 = f32[16,1,2]{2,1,0:T(1,128)S(1)} all-to-all(f32[16,1,2]{2,1,0:T(1,128)S(1)} %broadcast_in_dim.33), channel_id=1, replica_groups=mesh['tm'=32,'space'=16] {'space'}, dimensions={0} | all-to-all | bytes 256 | tf_op jit(solution)/shard_map/all_to_all | solution.py:16
  343.9 2.8 collective-permute-start.24
  346.7 2.1 collective-permute-start.23
  348.8 6.8 %collective-permute-done.23 = f32[1,32,128]{2,1,0:T(8,128)S(1)} collective-permute-done((f32[1,32,128]{2,1,0:T(8,128)S(1)}, f32[1,32,128]{2,1,0:T(8,128)S(1)}, u32[]{:S(2)}, u32[]{:S(2)}) %collective-permute-start.23) | collective-permute-done | bytes 16416 | tf_op jit(solution)/shard_map/ppermute | solution.py:43
  355.9 1.7 multiply_reduce_fusion.6
  358.9 18.4 %all_to_all.80 = f32[16,1,2]{2,1,0:T(1,128)S(1)} all-to-all(f32[16,1,2]{2,1,0:T(1,128)S(1)} %broadcast_in_dim.34), channel_id=1, replica_groups=mesh['tm'=32,'space'=16] {'space'}, dimensions={0} | all-to-all | bytes 256 | tf_op jit(solution)/shard_map/all_to_all | solution.py:16
  382.9 2.8 collective-permute-start.26
  385.6 1.9 collective-permute-start.25
  387.6 7.0 %collective-permute-done.25 = f32[1,32,128]{2,1,0:T(8,128)S(1)} collective-permute-done((f32[1,32,128]{2,1,0:T(8,128)S(1)}, f32[1,32,128]{2,1,0:T(8,128)S(1)}, u32[]{:S(2)}, u32[]{:S(2)}) %collective-permute-start.25) | collective-permute-done | bytes 16416 | tf_op jit(solution)/shard_map/ppermute | solution.py:43
  397.3 18.4 %all_to_all.81 = f32[16,1,2]{2,1,0:T(1,128)S(1)} all-to-all(f32[16,1,2]{2,1,0:T(1,128)S(1)} %broadcast_in_dim.35), channel_id=1, replica_groups=mesh['tm'=32,'space'=16] {'space'}, dimensions={0} | all-to-all | bytes 256 | tf_op jit(solution)/shard_map/all_to_all | solution.py:16
  420.2 2.8 collective-permute-start.28
  423.0 1.9 collective-permute-start.27
  424.9 7.0 %collective-permute-done.27 = f32[1,32,128]{2,1,0:T(8,128)S(1)} collective-permute-done((f32[1,32,128]{2,1,0:T(8,128)S(1)}, f32[1,32,128]{2,1,0:T(8,128)S(1)}, u32[]{:S(2)}, u32[]{:S(2)}) %collective-permute-start.27) | collective-permute-done | bytes 16416 | tf_op jit(solution)/shard_map/ppermute | solution.py:43
  432.2 1.7 multiply_reduce_fusion.2
  435.1 18.4 %all_to_all.82 = f32[16,1,2]{2,1,0:T(1,128)S(1)} all-to-all(f32[16,1,2]{2,1,0:T(1,128)S(1)} %broadcast_in_dim.36), channel_id=1, replica_groups=mesh['tm'=32,'space'=16] {'space'}, dimensions={0} | all-to-all | bytes 256 | tf_op jit(solution)/shard_map/all_to_all | solution.py:16
  459.0 2.8 collective-permute-start.30
  461.8 1.9 collective-permute-start.29
  463.7 7.0 %collective-permute-done.29 = f32[1,32,128]{2,1,0:T(8,128)S(1)} collective-permute-done((f32[1,32,128]{2,1,0:T(8,128)S(1)}, f32[1,32,128]{2,1,0:T(8,128)S(1)}, u32[]{:S(2)}, u32[]{:S(2)}) %collective-permute-start.29) | collective-permute-done | bytes 16416 | tf_op jit(solution)/shard_map/ppermute | solution.py:43
  472.1 1.4 pad_maximum_fusion.41
  473.5 18.4 %all_to_all.83 = f32[16,1,2]{2,1,0:T(1,128)S(1)} all-to-all(f32[16,1,2]{2,1,0:T(1,128)S(1)} %broadcast_in_dim.37), channel_id=1, replica_groups=mesh['tm'=32,'space'=16] {'space'}, dimensions={0} | all-to-all | bytes 256 | tf_op jit(solution)/shard_map/all_to_all | solution.py:16
  (126 shorter events, 40.5 us)
Async XLA Ops:
  0.0 18.2 %collective-permute-start = (f32[16,32,128]{2,1,0:T(8,128)}, f32[16,32,128]{2,1,0:T(8,128)S(1)}, u32[]{:S(2)}, u32[]{:S(2)}) collective-permute-start(f32[16,32,128]{2,1,0:T(8,128)} %bitcast.57), channel_id=1, source_target_pairs={{0,16},{16,32},{32,48},{48,64},{64,80},{80,96},{96,112},{112,128},... | collective-permute-start | bytes 786440 | tf_op jit(solution)/shard_map/ppermute | solution.py:53
  5.6 23.1 %collective-permute-start.3 = (f32[1,32,128]{2,1,0:T(8,128)S(1)}, f32[1,32,128]{2,1,0:T(8,128)S(1)}, u32[]{:S(2)}, u32[]{:S(2)}) collective-permute-start(f32[1,32,128]{2,1,0:T(8,128)S(1)} %get-tuple-element.74), channel_id=1, source_target_pairs={{0,1},{1,2},{2,3},{3,4},{4,5},{5,6},{6,7},{7,8},{8,9},{9,10},{10,1... | collective-permute-start | bytes 49160 | tf_op jit(solution)/shard_map/ppermute | solution.py:41
  16.1 12.6 %copy-start = (f32[16,32,128]{2,1,0:T(8,128)S(1)}, f32[16,32,128]{2,1,0:T(8,128)}, u32[]{:S(2)}) copy-start(f32[16,32,128]{2,1,0:T(8,128)} %param.6) | copy-start | bytes 786436
  16.2 12.6 %collective-permute-start.1 = (f32[1,32,128]{2,1,0:T(8,128)S(1)}, f32[1,32,128]{2,1,0:T(8,128)S(1)}, u32[]{:S(2)}, u32[]{:S(2)}) collective-permute-start(f32[1,32,128]{2,1,0:T(8,128)S(1)} %get-tuple-element.75), channel_id=1, source_target_pairs={{1,0},{2,1},{3,2},{4,3},{5,4},{6,5},{7,6},{8,7},{9,8},{10,9},{11,1... | collective-permute-start | bytes 49160 | tf_op jit(solution)/shard_map/ppermute | solution.py:43
  19.2 9.8 %collective-permute-start.4 = (f32[1,32,128]{2,1,0:T(8,128)S(1)}, f32[1,32,128]{2,1,0:T(8,128)S(1)}, u32[]{:S(2)}, u32[]{:S(2)}) collective-permute-start(f32[1,32,128]{2,1,0:T(8,128)S(1)} %get-tuple-element.76), channel_id=1, source_target_pairs={{0,1},{1,2},{2,3},{3,4},{4,5},{5,6},{6,7},{7,8},{8,9},{9,10},{10,1... | collective-permute-start | bytes 49160 | tf_op jit(solution)/shard_map/ppermute | solution.py:41
  26.8 9.0 %collective-permute-start.2 = (f32[1,32,128]{2,1,0:T(8,128)S(1)}, f32[1,32,128]{2,1,0:T(8,128)S(1)}, u32[]{:S(2)}, u32[]{:S(2)}) collective-permute-start(f32[1,32,128]{2,1,0:T(8,128)S(1)} %get-tuple-element.77), channel_id=1, source_target_pairs={{1,0},{2,1},{3,2},{4,3},{5,4},{6,5},{7,6},{8,7},{9,8},{10,9},{11,1... | collective-permute-start | bytes 49160 | tf_op jit(solution)/shard_map/ppermute | solution.py:43
  29.0 7.0 %copy-start.3 = (f32[16,32,128]{2,1,0:T(8,128)S(1)}, f32[16,32,128]{2,1,0:T(8,128)}, u32[]{:S(2)}) copy-start(f32[16,32,128]{2,1,0:T(8,128)} %param.7) | copy-start | bytes 786436
  36.6 4.3 collective-permute-start.6
  38.6 9.0 %collective-permute-start.5 = (f32[1,32,128]{2,1,0:T(8,128)S(1)}, f32[1,32,128]{2,1,0:T(8,128)S(1)}, u32[]{:S(2)}, u32[]{:S(2)}) collective-permute-start(f32[1,32,128]{2,1,0:T(8,128)S(1)} %get-tuple-element.73), channel_id=1, source_target_pairs={{1,0},{2,1},{3,2},{4,3},{5,4},{6,5},{7,6},{8,7},{9,8},{10,9},{11,1... | collective-permute-start | bytes 49160 | tf_op jit(solution)/shard_map/ppermute | solution.py:43
  67.4 4.7 collective-permute-start.8
  70.1 9.0 %collective-permute-start.7 = (f32[1,32,128]{2,1,0:T(8,128)S(1)}, f32[1,32,128]{2,1,0:T(8,128)S(1)}, u32[]{:S(2)}, u32[]{:S(2)}) collective-permute-start(f32[1,32,128]{2,1,0:T(8,128)S(1)} %get-tuple-element.71), channel_id=1, source_target_pairs={{1,0},{2,1},{3,2},{4,3},{5,4},{6,5},{7,6},{8,7},{9,8},{10,9},{11,1... | collective-permute-start | bytes 49160 | tf_op jit(solution)/shard_map/ppermute | solution.py:43
  105.5 4.7 collective-permute-start.10
  108.3 9.0 %collective-permute-start.9 = (f32[1,32,128]{2,1,0:T(8,128)S(1)}, f32[1,32,128]{2,1,0:T(8,128)S(1)}, u32[]{:S(2)}, u32[]{:S(2)}) collective-permute-start(f32[1,32,128]{2,1,0:T(8,128)S(1)} %get-tuple-element.69), channel_id=1, source_target_pairs={{1,0},{2,1},{3,2},{4,3},{5,4},{6,5},{7,6},{8,7},{9,8},{10,9},{11,1... | collective-permute-start | bytes 49160 | tf_op jit(solution)/shard_map/ppermute | solution.py:43
  144.5 4.7 collective-permute-start.12
  147.3 9.0 %collective-permute-start.11 = (f32[1,32,128]{2,1,0:T(8,128)S(1)}, f32[1,32,128]{2,1,0:T(8,128)S(1)}, u32[]{:S(2)}, u32[]{:S(2)}) collective-permute-start(f32[1,32,128]{2,1,0:T(8,128)S(1)} %get-tuple-element.67), channel_id=1, source_target_pairs={{1,0},{2,1},{3,2},{4,3},{5,4},{6,5},{7,6},{8,7},{9,8},{10,9},{11,1... | collective-permute-start | bytes 49160 | tf_op jit(solution)/shard_map/ppermute | solution.py:43
  157.5 36.3 %copy-start.1 = (f32[16,32,128]{2,1,0:T(8,128)}, f32[16,32,128]{2,1,0:T(8,128)S(1)}, u32[]{:S(2)}) copy-start(f32[16,32,128]{2,1,0:T(8,128)S(1)} %get-tuple-element.37) | copy-start | bytes 786436
  181.8 4.7 collective-permute-start.14
  184.6 9.0 %collective-permute-start.13 = (f32[1,32,128]{2,1,0:T(8,128)S(1)}, f32[1,32,128]{2,1,0:T(8,128)S(1)}, u32[]{:S(2)}, u32[]{:S(2)}) collective-permute-start(f32[1,32,128]{2,1,0:T(8,128)S(1)} %get-tuple-element.65), channel_id=1, source_target_pairs={{1,0},{2,1},{3,2},{4,3},{5,4},{6,5},{7,6},{8,7},{9,8},{10,9},{11,1... | collective-permute-start | bytes 49160 | tf_op jit(solution)/shard_map/ppermute | solution.py:43
  220.7 4.7 collective-permute-start.16
  223.4 9.0 %collective-permute-start.15 = (f32[1,32,128]{2,1,0:T(8,128)S(1)}, f32[1,32,128]{2,1,0:T(8,128)S(1)}, u32[]{:S(2)}, u32[]{:S(2)}) collective-permute-start(f32[1,32,128]{2,1,0:T(8,128)S(1)} %get-tuple-element.63), channel_id=1, source_target_pairs={{1,0},{2,1},{3,2},{4,3},{5,4},{6,5},{7,6},{8,7},{9,8},{10,9},{11,1... | collective-permute-start | bytes 49160 | tf_op jit(solution)/shard_map/ppermute | solution.py:43
  258.4 4.8 collective-permute-start.18
  261.2 9.4 %copy-start.4 = (f32[16,32,128]{2,1,0:T(8,128)S(1)}, f32[16,32,128]{2,1,0:T(8,128)}, u32[]{:S(2)}) copy-start(f32[16,32,128]{2,1,0:T(8,128)} %param.7) | copy-start | bytes 786436
  261.2 9.1 %collective-permute-start.17 = (f32[1,32,128]{2,1,0:T(8,128)S(1)}, f32[1,32,128]{2,1,0:T(8,128)S(1)}, u32[]{:S(2)}, u32[]{:S(2)}) collective-permute-start(f32[1,32,128]{2,1,0:T(8,128)S(1)} %get-tuple-element.61), channel_id=1, source_target_pairs={{1,0},{2,1},{3,2},{4,3},{5,4},{6,5},{7,6},{8,7},{9,8},{10,9},{11,1... | collective-permute-start | bytes 49160 | tf_op jit(solution)/shard_map/ppermute | solution.py:43
  271.0 4.3 collective-permute-start.20
  272.9 9.7 %collective-permute-start.19 = (f32[1,32,128]{2,1,0:T(8,128)S(1)}, f32[1,32,128]{2,1,0:T(8,128)S(1)}, u32[]{:S(2)}, u32[]{:S(2)}) collective-permute-start(f32[1,32,128]{2,1,0:T(8,128)S(1)} %get-tuple-element.59), channel_id=1, source_target_pairs={{1,0},{2,1},{3,2},{4,3},{5,4},{6,5},{7,6},{8,7},{9,8},{10,9},{11,1... | collective-permute-start | bytes 49160 | tf_op jit(solution)/shard_map/ppermute | solution.py:43
  305.8 4.7 collective-permute-start.22
  308.6 9.0 %collective-permute-start.21 = (f32[1,32,128]{2,1,0:T(8,128)S(1)}, f32[1,32,128]{2,1,0:T(8,128)S(1)}, u32[]{:S(2)}, u32[]{:S(2)}) collective-permute-start(f32[1,32,128]{2,1,0:T(8,128)S(1)} %get-tuple-element.57), channel_id=1, source_target_pairs={{1,0},{2,1},{3,2},{4,3},{5,4},{6,5},{7,6},{8,7},{9,8},{10,9},{11,1... | collective-permute-start | bytes 49160 | tf_op jit(solution)/shard_map/ppermute | solution.py:43
  343.9 4.9 collective-permute-start.24
  346.7 9.0 %collective-permute-start.23 = (f32[1,32,128]{2,1,0:T(8,128)S(1)}, f32[1,32,128]{2,1,0:T(8,128)S(1)}, u32[]{:S(2)}, u32[]{:S(2)}) collective-permute-start(f32[1,32,128]{2,1,0:T(8,128)S(1)} %get-tuple-element.55), channel_id=1, source_target_pairs={{1,0},{2,1},{3,2},{4,3},{5,4},{6,5},{7,6},{8,7},{9,8},{10,9},{11,1... | collective-permute-start | bytes 49160 | tf_op jit(solution)/shard_map/ppermute | solution.py:43
  382.9 4.7 collective-permute-start.26
  385.6 9.0 %collective-permute-start.25 = (f32[1,32,128]{2,1,0:T(8,128)S(1)}, f32[1,32,128]{2,1,0:T(8,128)S(1)}, u32[]{:S(2)}, u32[]{:S(2)}) collective-permute-start(f32[1,32,128]{2,1,0:T(8,128)S(1)} %get-tuple-element.53), channel_id=1, source_target_pairs={{1,0},{2,1},{3,2},{4,3},{5,4},{6,5},{7,6},{8,7},{9,8},{10,9},{11,1... | collective-permute-start | bytes 49160 | tf_op jit(solution)/shard_map/ppermute | solution.py:43
  395.9 36.3 %copy-start.2 = (f32[16,32,128]{2,1,0:T(8,128)}, f32[16,32,128]{2,1,0:T(8,128)S(1)}, u32[]{:S(2)}) copy-start(f32[16,32,128]{2,1,0:T(8,128)S(1)} %get-tuple-element.30) | copy-start | bytes 786436
  420.2 4.7 collective-permute-start.28
  423.0 9.0 %collective-permute-start.27 = (f32[1,32,128]{2,1,0:T(8,128)S(1)}, f32[1,32,128]{2,1,0:T(8,128)S(1)}, u32[]{:S(2)}, u32[]{:S(2)}) collective-permute-start(f32[1,32,128]{2,1,0:T(8,128)S(1)} %get-tuple-element.51), channel_id=1, source_target_pairs={{1,0},{2,1},{3,2},{4,3},{5,4},{6,5},{7,6},{8,7},{9,8},{10,9},{11,1... | collective-permute-start | bytes 49160 | tf_op jit(solution)/shard_map/ppermute | solution.py:43
  459.0 4.7 collective-permute-start.30
  461.8 9.0 %collective-permute-start.29 = (f32[1,32,128]{2,1,0:T(8,128)S(1)}, f32[1,32,128]{2,1,0:T(8,128)S(1)}, u32[]{:S(2)}, u32[]{:S(2)}) collective-permute-start(f32[1,32,128]{2,1,0:T(8,128)S(1)} %get-tuple-element.49), channel_id=1, source_target_pairs={{1,0},{2,1},{3,2},{4,3},{5,4},{6,5},{7,6},{8,7},{9,8},{10,9},{11,1... | collective-permute-start | bytes 49160 | tf_op jit(solution)/shard_map/ppermute | solution.py:43
where the time goes:
time: 500 us; the launch traced here: 498 us
  blocking collectives  217 us (43%)
  waiting for transfers between devices  97.7 us (20%)
  starting transfers between devices  87.3 us (17%)
  between operations  43.7 us (9%)
  other arithmetic  43.4 us (9%)
  local copies, waits for them, and re-layouts  7.97 us (2%)
    all_to_all x12, blocking collectives, copy_for_each(): lax.all_to_all(jnp.broadcast_to(array[None], (devices, *array.shape)), ax...  217 us
    ppermute x15, waiting for transfers between devices, extended(): lax.ppermute(head, axis, [((i + 1) % count, i) for i in range(ends)])  97.7 us
    ppermute x15, starting transfers between devices, extended(): lax.ppermute(tail, axis, [(i, (i + 1) % count) for i in range(ends)])  52.3 us
    ppermute x15, starting transfers between devices, extended(): lax.ppermute(head, axis, [((i + 1) % count, i) for i in range(ends)])  30.2 us
    concatenate x12, other arithmetic, packed_total(): subtotal = over_copies(jnp.concatenate([a.ravel() for a in arrays]), axis)  16.1 us
    reduce_sum x12, other arithmetic, pair_sums(): jnp.sum(residual * residual)  15.1 us
  transfers between devices with their start and end apart: 31, of which 14 were waited for; matrix products, arithmetic and copies ran while one was open for 0% of the time, Pallas kernels for 0%

commit v1 on v0

v1 whole, which is shorter than its diff:
```python
import functools

import jax
import jax.numpy as jnp
from jax import lax
from jax.experimental import pallas as pl
from jax.experimental.pallas import tpu as pltpu
from jax.sharding import PartitionSpec as P

MESH = pl.DeviceIdType.MESH
f32 = jnp.float32

NEAR = 7
FAR = 6
HD = NEAR + FAR
SC = 1.0 / 128.0
TOL = 1e-7


def loop(lo, hi, body, init, unroll):
    n = hi - lo
    while n % unroll:
        unroll -= 1
    return lax.fori_loop(lo, hi, body, init, unroll=unroll)


def gauss_jordan(m, n):
    rows = lax.broadcasted_iota(jnp.int32, (8, 128), 0)
    first = m
    for k in range(n):
        row = jnp.broadcast_to(m[k : k + 1, :], (8, 128))
        col = jnp.broadcast_to(m[:, k : k + 1], (8, 128))
        pivot = jnp.broadcast_to(row[:, k : k + 1], (8, 128))
        size = jnp.broadcast_to(jnp.broadcast_to(first[k : k + 1, :], (8, 128))[:, k : k + 1], (8, 128))
        good = pivot > TOL * size
        inverse = jnp.where(good, 1.0 / jnp.where(good, pivot, 1.0), 0.0)
        row = row * inverse
        m = jnp.where(rows == k, row, m - col * row)
    return jnp.broadcast_to(m[:, 6:7], (8, 128))


def kernel(ns, nt, nz, cp_hbm, co_hbm, cond_hbm, force_hbm, out_hbm, X, C, F, WZ, WY, WX, E, V, W, CP, CO, CR, O,
           row_buf, gather, load_sem, out_sem, halo_send, halo_recv, shift_send, shift_recv, ar_send, ar_recv):
    ny, nx = X.shape[1:]
    s = lax.axis_index("space")
    t = lax.axis_index("tm")
    a, b = HD, HD + nz
    has_left, has_right = s > 0, s < ns - 1

    loads = [
        pltpu.make_async_copy(co_hbm, CO, load_sem.at[0]),
        pltpu.make_async_copy(cond_hbm, C.at[pl.ds(a, nz)], load_sem.at[1]),
        pltpu.make_async_copy(force_hbm, F.at[pl.ds(a, nz)], load_sem.at[2]),
        pltpu.make_async_copy(cp_hbm, CP, load_sem.at[3]),
    ]
    for c in loads:
        c.start()

    barrier = pltpu.get_barrier_semaphore()
    for d in range(1, ns):
        pl.semaphore_signal(barrier, inc=1, device_id={"space": lax.rem(s + d, ns)}, device_id_type=MESH)

    @pl.when(t > 0)
    def _():
        pl.semaphore_signal(barrier, inc=1, device_id={"tm": lax.rem(t + nt - 1, nt)}, device_id_type=MESH)

    @pl.when(t < nt - 1)
    def _():
        pl.semaphore_signal(barrier, inc=1, device_id={"tm": lax.rem(t + 1, nt)}, device_id_type=MESH)

    zero = jnp.zeros((ny, nx), f32)

    def clear(lo, hi):
        def body(k, carry):
            X[k] = zero
            C[k] = zero
            F[k] = zero
            return carry

        lax.fori_loop(lo, hi, body, 0)

    @pl.when(jnp.logical_not(has_left))
    def _():
        clear(0, a)

    @pl.when(jnp.logical_not(has_right))
    def _():
        clear(b, b + HD)

    @pl.when(t == 0)
    def _():
        def body(k, carry):
            CR[k] = zero
            return carry

        lax.fori_loop(0, nz, body, 0)

    pl.semaphore_wait(barrier, (ns - 1) + (t > 0).astype(jnp.int32) + (t < nt - 1).astype(jnp.int32))

    shift = pltpu.make_async_remote_copy(
        CO, CR, shift_send, shift_recv, device_id={"tm": lax.rem(t + 1, nt)}, device_id_type=MESH
    )

    def halo(field, far, side):
        ref = (X, C, F)[field]
        near = NEAR - 1 if field == 2 else NEAR
        n = FAR if far else near
        if side == 0:
            src = b - near - FAR if far else b - near
            dst = a - near - FAR if far else a - near
            to = lax.rem(s + 1, ns)
        else:
            src = a + near if far else a
            dst = b + near if far else b
            to = lax.rem(s + ns - 1, ns)
        i = field * 4 + far * 2 + side
        return pltpu.make_async_remote_copy(
            ref.at[pl.ds(src, n)], ref.at[pl.ds(dst, n)], halo_send.at[i], halo_recv.at[i],
            device_id={"space": to}, device_id_type=MESH,
        )

    def send_halo(fields, far):
        @pl.when(has_right)
        def _():
            for f in fields:
                halo(f, far, 0).start()

        @pl.when(has_left)
        def _():
            for f in fields:
                halo(f, far, 1).start()

    def wait_halo(fields, far, sent):
        @pl.when(has_right if sent else has_left)
        def _():
            for f in fields:
                c = halo(f, far, 0)
                c.wait_send() if sent else c.wait_recv()

        @pl.when(has_left if sent else has_right)
        def _():
            for f in fields:
                c = halo(f, far, 1)
                c.wait_send() if sent else c.wait_recv()

    loads[0].wait()

    @pl.when(t < nt - 1)
    def _():
        shift.start()

    loads[1].wait()
    loads[2].wait()
    send_halo((1, 2), 0)

    edge_y = lax.broadcasted_iota(jnp.int32, (ny, nx), 0)
    edge_x = lax.broadcasted_iota(jnp.int32, (ny, nx), 1)
    outer = ((edge_y == 0).astype(f32) + (edge_y == ny - 1).astype(f32)
             + (edge_x == 0).astype(f32) + (edge_x == nx - 1).astype(f32))
    keep_y = (edge_y < ny - 1).astype(f32) * (2 * SC)
    keep_x = (edge_x < nx - 1).astype(f32) * (2 * SC)
    outer = outer * (2 * SC)

    def plane_weights(lo, hi):
        def body(k, carry):
            c = C[k]
            WY[k] = keep_y * (c + pltpu.roll(c, ny - 1, 0))
            WX[k] = keep_x * (c + pltpu.roll(c, nx - 1, 1))
            E[k] = SC + outer * c
            return carry

        loop(lo, hi, body, 0, 2)

    def face_weights(lo, hi):
        def body(k, carry):
            WZ[k] = (2 * SC) * (C[k - 1] + C[k])
            return carry

        loop(lo, hi, body, 0, 2)

    def apply(src, dst, lo, hi, finish=None):
        def body(k, below):
            v = src(k)
            above = WZ[k + 1] * (src(k + 1) - v)
            fy = WY[k] * (pltpu.roll(v, ny - 1, 0) - v)
            fx = WX[k] * (pltpu.roll(v, nx - 1, 1) - v)
            out = E[k] * v - ((above - below) + (fy - pltpu.roll(fy, 1, 0)) + (fx - pltpu.roll(fx, 1, 1)))
            dst(k, out, v)
            return above

        loop(lo, hi, body, WZ[lo] * (src(lo) - src(lo - 1)), 2)

    def from_x(k):
        return X[k]

    def start_residual(k, image, v):
        V[0, k] = (v + 0.25 * F[k]) - 128.0 * image

    def power(buf, j, lo, hi):
        def put(k, image, v):
            buf[j, k] = image

        apply(lambda k: buf[j - 1, k], put, lo, hi)

    def dots(pairs, used):
        def body(k, accs):
            val = {u: (V if u[0] == "v" else W)[int(u[1]), k] for u in used}
            out = []
            for acc, (p, q) in zip(accs, pairs):
                z = val[p] * val[q]
                out.append(acc + ((z[0:8] + z[8:16]) + (z[16:24] + z[24:32])))
            return tuple(out)

        return loop(a, b, body, tuple(jnp.zeros((8, nx), f32) for _ in pairs), 2)

    lane = lax.broadcasted_iota(jnp.int32, (1, 128), 1)

    def to_row(pairs, places, accs):
        r = jnp.zeros((1, 128), f32)
        for pair, acc in zip(pairs, accs):
            total = jnp.sum(jnp.sum(acc, axis=0, keepdims=True), axis=1, keepdims=True)
            mask = None
            for i, j in places[pair]:
                m = lane == (j - 8 * i) % 128
                mask = m if mask is None else jnp.logical_or(mask, m)
            r = jnp.where(mask, jnp.broadcast_to(total, (1, 128)), r)
        return r

    def exchange(n, d):
        return pltpu.make_async_remote_copy(
            row_buf.at[n], gather.at[n, s], ar_send.at[n, d - 1], ar_recv.at[n, d - 1],
            device_id={"space": lax.rem(s + d, ns)}, device_id_type=MESH,
        )

    order = sorted(range(1, ns), key=lambda d: -min(d, ns - d))

    def send_row(n, r):
        row_buf[n] = r
        for d in order:
            exchange(n, d).start()

    def total_tile(n, r):
        for d in order:
            exchange(n, d).wait()
        parts = [jnp.where(s == q, r, gather[n, q]) for q in range(ns)]
        while len(parts) > 1:
            parts = [parts[i] + parts[i + 1] for i in range(0, len(parts), 2)]
        return pltpu.roll(jnp.broadcast_to(parts[0], (8, 128)), 0, 1, stride=8, stride_axis=0)

    first_pairs = (("v0", "v0"), ("v0", "v1"), ("v0", "v2"), ("v1", "v1"), ("v1", "v2"), ("v2", "v2"), ("v2", "v3"))
    first_places = {
        ("v0", "v0"): ((0, 6),), ("v0", "v1"): ((0, 0), (1, 6)), ("v0", "v2"): ((2, 6),),
        ("v1", "v1"): ((1, 0), (0, 1)), ("v1", "v2"): ((1, 1), (2, 0), (0, 2)),
        ("v2", "v2"): ((2, 1), (1, 2)), ("v2", "v3"): ((2, 2),),
    }
    second_pairs = [("w0", "v0")] + [(f"w{i}", f"v{j}") for i in range(3) for j in (1, 2, 3)]
    second_places = {("w0", "v0"): ((0, 6),)}
    for i in range(3):
        for j in range(3):
            second_places[(f"w{i}", f"v{j + 1}")] = ((3 + i, j), (j, 3 + i))
    second_places[("w0", "v1")] += ((1, 6),)
    second_places[("w0", "v2")] += ((2, 6),)
    for pair, where in first_places.items():
        q = tuple(p.replace("v", "w") for p in pair)
        second_pairs.append(q)
        second_places[q] = tuple((i + 3, j if j == 6 else j + 3) for i, j in where)

    def spread(y, j):
        return jnp.broadcast_to(y[j : j + 1, :], (ny, nx))

    def next_residual(coefs, lo, hi):
        def body(k, carry):
            W[0, k] = V[0, k] - (coefs[0] * V[1, k] + coefs[1] * V[2, k] + coefs[2] * V[3, k])
            return carry

        loop(lo, hi, body, 0, 2)

    def section(which):
        lo, hi = lambda d: a - d, lambda d: b + d
        apply(from_x, start_residual, lo(6), hi(6))
        for j in (1, 2, 3):
            power(V, j, lo(6 - j), hi(6 - j))
        r = to_row(first_pairs, first_places, dots(first_pairs, ("v0", "v1", "v2", "v3")))
        send_row(2 * which, r)
        tile = total_tile(2 * which, r)
        y1 = gauss_jordan(tile, 3)
        coefs = [spread(y1, j) for j in range(3)]
        next_residual(coefs, lo(3), hi(3))
        for j in (1, 2, 3):
            power(W, j, lo(3 - j), hi(3 - j))
        r = to_row(second_pairs, second_places,
                   dots(second_pairs, ("v0", "v1", "v2", "v3", "w0", "w1", "w2", "w3")))
        send_row(2 * which + 1, r)
        if which == 0:
            wait_halo((1, 2, 0), 1, False)
            plane_weights(a - 12, a - 6)
            plane_weights(b + 6, b + 12)
            face_weights(a - 12, a - 6)
            face_weights(b + 7, b + 13)
            apply(from_x, start_residual, lo(12), lo(6))
            apply(from_x, start_residual, hi(6), hi(12))
            for j in (1, 2, 3):
                power(V, j, lo(12 - j), lo(6 - j))
                power(V, j, hi(6 - j), hi(12 - j))
            next_residual(coefs, lo(9), lo(3))
            next_residual(coefs, hi(3), hi(9))
            for j in (1, 2):
                power(W, j, lo(9 - j), lo(3 - j))
                power(W, j, hi(3 - j), hi(9 - j))
        rows = lax.broadcasted_iota(jnp.int32, (8, 128), 0)
        lanes = lax.broadcasted_iota(jnp.int32, (8, 128), 1)
        old = jnp.logical_and(jnp.logical_and(rows < 3, lanes < 3), rows >= 0)
        tile2 = jnp.where(old, tile, total_tile(2 * which + 1, r))
        y2 = gauss_jordan(tile2, 6)
        both = [(y1 + y2) * SC, y2 * SC]
        cv = [spread(both[0], j) for j in range(3)]
        cw = [spread(both[1], 3 + j) for j in range(3)]

        def result(k):
            v = (cv[0] * V[0, k] + cv[1] * V[1, k]) + cv[2] * V[2, k]
            w = (cw[0] * W[0, k] + cw[1] * W[1, k]) + cw[2] * W[2, k]
            return X[k] + (v + w)

        return result

    loads[3].wait()

    @pl.when(t > 0)
    def _():
        shift.wait_recv()

    def add(k, carry):
        X[a + k] = CP[k] + CR[k]
        return carry

    loop(0, nz, add, 0, 4)
    send_halo((0,), 0)
    send_halo((1, 2, 0), 1)

    wait_halo((1, 2), 0, False)
    plane_weights(a - 6, b + 6)
    face_weights(a - 6, b + 7)

    @pl.when(jnp.logical_not(has_left))
    def _():
        WZ[a] = zero
        E[a] = E[a] + (2 * SC) * C[a]

    @pl.when(jnp.logical_not(has_right))
    def _():
        WZ[b] = zero
        E[b - 1] = E[b - 1] + (2 * SC) * C[b - 1]

    wait_halo((0,), 0, False)

    result = section(0)
    wait_halo((0,), 0, True)
    wait_halo((0,), 1, True)

    def put_x(k, carry):
        X[k] = result(k)
        return carry

    loop(a - 7, b + 7, put_x, 0, 2)
    out0 = pltpu.make_async_copy(X.at[pl.ds(a, nz)], out_hbm.at[0], out_sem.at[0])
    out0.start()
    result = section(1)

    def put_o(k, carry):
        O[k] = result(a + k)
        return carry

    loop(0, nz, put_o, 0, 2)
    out1 = pltpu.make_async_copy(O, out_hbm.at[1], out_sem.at[1])
    out1.start()

    wait_halo((1, 2), 0, True)
    wait_halo((1, 2), 1, True)

    @pl.when(t < nt - 1)
    def _():
        shift.wait_send()

    out0.wait()
    out1.wait()


def solution(mesh):
    ns, nt = mesh.shape["space"], mesh.shape["tm"]

    def body(c_points, corrections, conductivity, forcing):
        nz, ny, nx = conductivity.shape
        ext = nz + 2 * HD
        out = pl.pallas_call(
            functools.partial(kernel, ns, nt, nz),
            out_shape=jax.ShapeDtypeStruct((2, nz, ny, nx), f32),
            in_specs=[pl.BlockSpec(memory_space=pl.ANY)] * 4,
            out_specs=pl.BlockSpec(memory_space=pl.ANY),
            scratch_shapes=[
                pltpu.VMEM((ext, ny, nx), f32),
                pltpu.VMEM((ext, ny, nx), f32),
                pltpu.VMEM((ext, ny, nx), f32),
                pltpu.VMEM((ext + 1, ny, nx), f32),
                pltpu.VMEM((ext, ny, nx), f32),
                pltpu.VMEM((ext, ny, nx), f32),
                pltpu.VMEM((ext, ny, nx), f32),
                pltpu.VMEM((4, ext, ny, nx), f32),
                pltpu.VMEM((4, ext, ny, nx), f32),
                pltpu.VMEM((nz, ny, nx), f32),
                pltpu.VMEM((nz, ny, nx), f32),
                pltpu.VMEM((nz, ny, nx), f32),
                pltpu.VMEM((nz, ny, nx), f32),
                pltpu.VMEM((4, 1, 128), f32),
                pltpu.VMEM((4, ns, 1, 128), f32),
                pltpu.SemaphoreType.DMA((4,)),
                pltpu.SemaphoreType.DMA((2,)),
                pltpu.SemaphoreType.DMA((12,)),
                pltpu.SemaphoreType.DMA((12,)),
                pltpu.SemaphoreType.DMA,
                pltpu.SemaphoreType.DMA,
                pltpu.SemaphoreType.DMA((4, ns - 1)),
                pltpu.SemaphoreType.DMA((4, ns - 1)),
            ],
            compiler_params=pltpu.CompilerParams(collective_id=0, has_side_effects=True),
        )(c_points[0], corrections[0], conductivity, forcing)
        return out[None]

    in_specs = (
        P("tm", "space", None, None),
        P("tm", "space", None, None),
        P("space", None, None),
        P("space", None, None),
    )
    out_specs = P("tm", None, "space", None, None)
    return jax.shard_map(body, mesh=mesh, in_specs=in_specs, out_specs=out_specs, check_vma=False)
```

time: 500 us -> 105 us (0.21)
  the two profiles are of different devices: /device:TPU:1 before, /device:TPU:160 now
where the time goes in v1:
time: 105 us; the launch traced here: 104 us
  Pallas kernels  102 us (97%)
  local copies, waits for them, and re-layouts  1.87 us (2%)
    pallas_call x1, Pallas kernels, body(): pl.pallas_call(functools.partial(kernel, ns, nt, nz), out_shape=jax.Shape...  102 us

profile of v1, /device:TPU:160, one launch (start us, length us, event | category | flops | bytes accessed | tf_op | source)
XLA Modules:
  0.0 104.4 jit_solution(14073923110951354527)
XLA Ops:
  0.0 102.5 %shard_map.46 = f32[2,16,32,128]{3,2,1,0:T(8,128)} custom-call(f32[16,32,128]{2,1,0:T(8,128)} %bitcast.4, f32[16,32,128]{2,1,0:T(8,128)} %bitcast.5, f32[16,32,128]{2,1,0:T(8,128)} %cond_hbm.1, f32[16,32,128]{2,1,0:T(8,128)} %force_hbm.1), custom_call_target="tpu_custom_call" | custom-call | tf_op jit(solution)/shard_map/pallas_call | solution.py:394
  102.5 1.9 %copy.6 = f32[1,2,16,32,128]{4,3,2,1,0:T(8,128)} copy(f32[1,2,16,32,128]{4,3,2,1,0:T(8,128)} %bitcast.3) | data formatting | bytes 1048576

commit v2 on v1

--- a/solution.py
+++ b/solution.py
@@ -282,6 +282,8 @@
             power(V, j, lo(6 - j), hi(6 - j))
         r = to_row(first_pairs, first_places, dots(first_pairs, ("v0", "v1", "v2", "v3")))
         send_row(2 * which, r)
+        if which == 0:
+            send_halo((1, 2, 0), 1)
         tile = total_tile(2 * which, r)
         y1 = gauss_jordan(tile, 3)
         coefs = [spread(y1, j) for j in range(3)]
@@ -335,7 +337,6 @@
 
     loop(0, nz, add, 0, 4)
     send_halo((0,), 0)
-    send_halo((1, 2, 0), 1)
 
     wait_halo((1, 2), 0, False)
     plane_weights(a - 6, b + 6)

time: 105 us -> 94 us (0.90)
  the two profiles are of different devices: /device:TPU:160 before, /device:TPU:88 now
where the time goes in v2:
time: 94 us; the launch traced here: 93.8 us
  Pallas kernels  92 us (98%)
  local copies, waits for them, and re-layouts  1.87 us (2%)
    pallas_call x1, Pallas kernels, body(): pl.pallas_call(functools.partial(kernel, ns, nt, nz), out_shape=jax.Shape...  92 us

profile of v2, /device:TPU:88, one launch (start us, length us, event | category | flops | bytes accessed | tf_op | source)
XLA Modules:
  0.0 93.8 jit_solution(9273516351788002682)
XLA Ops:
  0.0 92.0 %shard_map.46 = f32[2,16,32,128]{3,2,1,0:T(8,128)} custom-call(f32[16,32,128]{2,1,0:T(8,128)} %bitcast.4, f32[16,32,128]{2,1,0:T(8,128)} %bitcast.5, f32[16,32,128]{2,1,0:T(8,128)} %cond_hbm.1, f32[16,32,128]{2,1,0:T(8,128)} %force_hbm.1), custom_call_target="tpu_custom_call" | custom-call | tf_op jit(solution)/shard_map/pallas_call | solution.py:395
  92.0 1.9 %copy.6 = f32[1,2,16,32,128]{4,3,2,1,0:T(8,128)} copy(f32[1,2,16,32,128]{4,3,2,1,0:T(8,128)} %bitcast.3) | data formatting | bytes 1048576

commit v3 on v2

--- a/solution.py
+++ b/solution.py
@@ -10,18 +10,23 @@
 MESH = pl.DeviceIdType.MESH
 f32 = jnp.float32
 
-NEAR = 7
-FAR = 6
-HD = NEAR + FAR
+LEVELS = ((0, 4), (4, 7), (7, 13))
+FORCE_LEVELS = ((0, 3), (3, 6), (6, 12))
+HD = 13
+SHARE = 4
+ALONG_Z = 4
 SC = 1.0 / 128.0
 TOL = 1e-7
+APPLY = 28
 
 
 def loop(lo, hi, body, init, unroll):
     n = hi - lo
-    while n % unroll:
-        unroll -= 1
-    return lax.fori_loop(lo, hi, body, init, unroll=unroll)
+    if n <= unroll:
+        return lax.fori_loop(lo, hi, body, init, unroll=n)
+    rest = n % unroll
+    init = lax.fori_loop(lo, hi - rest, body, init, unroll=unroll)
+    return lax.fori_loop(hi - rest, hi, body, init, unroll=rest) if rest else init
 
 
 def gauss_jordan(m, n):
@@ -39,8 +44,8 @@
     return jnp.broadcast_to(m[:, 6:7], (8, 128))
 
 
-def kernel(ns, nt, nz, cp_hbm, co_hbm, cond_hbm, force_hbm, out_hbm, X, C, F, WZ, WY, WX, E, V, W, CP, CO, CR, O,
-           row_buf, gather, load_sem, out_sem, halo_send, halo_recv, shift_send, shift_recv, ar_send, ar_recv):
+def kernel(ns, nt, nz, cp_hbm, co_hbm, cond_hbm, force_hbm, out_hbm, X, C, F, WZ, WY, WX, WL, E, V, W, CP, CO, CR, O,
+           row_buf, gather, load_sem, out_sem, halo_send, halo_recv, chip_send, chip_recv, far_send, far_recv, share_send, share_recv, shift_send, shift_recv, ar_send, ar_recv):
     ny, nx = X.shape[1:]
     s = lax.axis_index("space")
     t = lax.axis_index("tm")
@@ -68,6 +73,15 @@
     def _():
         pl.semaphore_signal(barrier, inc=1, device_id={"tm": lax.rem(t + 1, nt)}, device_id_type=MESH)
 
+    quarter = t // ALONG_Z
+
+    def sharer(d):
+        first = quarter - lax.rem(quarter, SHARE)
+        return (first + lax.rem(quarter + d, SHARE)) * ALONG_Z + lax.rem(t, ALONG_Z)
+
+    for d in range(1, SHARE):
+        pl.semaphore_signal(barrier, inc=1, device_id={"tm": sharer(d)}, device_id_type=MESH)
+
     zero = jnp.zeros((ny, nx), f32)
 
     def clear(lo, hi):
@@ -95,63 +109,138 @@
 
         lax.fori_loop(0, nz, body, 0)
 
-    pl.semaphore_wait(barrier, (ns - 1) + (t > 0).astype(jnp.int32) + (t < nt - 1).astype(jnp.int32))
-
-    shift = pltpu.make_async_remote_copy(
-        CO, CR, shift_send, shift_recv, device_id={"tm": lax.rem(t + 1, nt)}, device_id_type=MESH
-    )
-
-    def halo(field, far, side):
-        ref = (X, C, F)[field]
-        near = NEAR - 1 if field == 2 else NEAR
-        n = FAR if far else near
+    pl.semaphore_wait(barrier, (ns - 1) + (SHARE - 1) + (t > 0).astype(jnp.int32) + (t < nt - 1).astype(jnp.int32))
+
+    edge = LEVELS[0][1]
+    pieces = ((0, edge), (nz - edge, edge), (edge, nz - 2 * edge))
+
+    def shift(i):
+        p = pl.ds(*pieces[i])
+        return pltpu.make_async_remote_copy(
+            CO.at[p], CR.at[p], shift_send.at[i], shift_recv.at[i],
+            device_id={"tm": lax.rem(t + 1, nt)}, device_id_type=MESH,
+        )
+
+    def halo(level, side):
+        d0, d1 = LEVELS[level]
         if side == 0:
-            src = b - near - FAR if far else b - near
-            dst = a - near - FAR if far else a - near
-            to = lax.rem(s + 1, ns)
+            src, dst, to = b - d1, a - d1, lax.rem(s + 1, ns)
         else:
-            src = a + near if far else a
-            dst = b + near if far else b
-            to = lax.rem(s + ns - 1, ns)
-        i = field * 4 + far * 2 + side
+            src, dst, to = a + d0, b + d0, lax.rem(s + ns - 1, ns)
+        i = level * 2 + side
         return pltpu.make_async_remote_copy(
-            ref.at[pl.ds(src, n)], ref.at[pl.ds(dst, n)], halo_send.at[i], halo_recv.at[i],
+            X.at[pl.ds(src, d1 - d0)], X.at[pl.ds(dst, d1 - d0)], halo_send.at[i], halo_recv.at[i],
             device_id={"space": to}, device_id_type=MESH,
         )
 
-    def send_halo(fields, far):
+    def send_halo(level):
         @pl.when(has_right)
         def _():
-            for f in fields:
-                halo(f, far, 0).start()
+            halo(level, 0).start()
 
         @pl.when(has_left)
         def _():
-            for f in fields:
-                halo(f, far, 1).start()
-
-    def wait_halo(fields, far, sent):
+            halo(level, 1).start()
+
+    def wait_halo(level, sent):
         @pl.when(has_right if sent else has_left)
         def _():
-            for f in fields:
-                c = halo(f, far, 0)
-                c.wait_send() if sent else c.wait_recv()
+            c = halo(level, 0)
+            c.wait_send() if sent else c.wait_recv()
 
         @pl.when(has_left if sent else has_right)
         def _():
-            for f in fields:
-                c = halo(f, far, 1)
-                c.wait_send() if sent else c.wait_recv()
-
-    loads[0].wait()
-
-    @pl.when(t < nt - 1)
-    def _():
-        shift.start()
+            c = halo(level, 1)
+            c.wait_send() if sent else c.wait_recv()
+
+    odd = lax.rem(s, 2)
+    outside = jnp.logical_and(has_left, has_right)
+    depths = ((LEVELS[0], (LEVELS[1][0], LEVELS[2][1])), (FORCE_LEVELS[0], (FORCE_LEVELS[1][0], FORCE_LEVELS[2][1])))
+    my_rows = pl.ds(pl.multiple_of(lax.rem(quarter, SHARE) * (ny // SHARE), 8), ny // SHARE)
+
+    def chip_copy(field, part):
+        d0, d1 = depths[field][part]
+        ref = (C, F)[field]
+        src = odd * (a + d0) + (1 - odd) * (b - d1)
+        dst = odd * (b + d0) + (1 - odd) * (a - d1)
+        i = field * 2 + part
+        return pltpu.make_async_remote_copy(
+            ref.at[pl.ds(src, d1 - d0)], ref.at[pl.ds(dst, d1 - d0)], chip_send.at[i], chip_recv.at[i],
+            device_id={"space": s + 1 - 2 * odd}, device_id_type=MESH,
+        )
+
+    def far_copy(field, part):
+        d0, d1 = depths[field][part]
+        ref = (C, F)[field]
+        src = odd * (b - d1) + (1 - odd) * (a + d0)
+        dst = odd * (a - d1) + (1 - odd) * (b + d0)
+        i = field * 2 + part
+        return pltpu.make_async_remote_copy(
+            ref.at[pl.ds(src, d1 - d0), my_rows], ref.at[pl.ds(dst, d1 - d0), my_rows], far_send.at[i], far_recv.at[i],
+            device_id={"space": lax.rem(s + ns - 1 + 2 * odd, ns)}, device_id_type=MESH,
+        )
+
+    def share_copy(field, part, d):
+        d0, d1 = depths[field][part]
+        ref = (C, F)[field]
+        here = odd * (b + d0) + (1 - odd) * (a - d1)
+        p = ref.at[pl.ds(here, d1 - d0), my_rows]
+        i = (field * 2 + part) * (SHARE - 1) + d - 1
+        return pltpu.make_async_remote_copy(
+            p, p, share_send.at[i], share_recv.at[i], device_id={"tm": sharer(d)}, device_id_type=MESH
+        )
+
+    def send_inputs(part):
+        for f in range(2):
+            chip_copy(f, part).start()
+
+        @pl.when(outside)
+        def _():
+            for f in range(2):
+                far_copy(f, part).start()
+
+    def pass_inputs(part):
+        @pl.when(outside)
+        def _():
+            for f in range(2):
+                far_copy(f, part).wait_recv()
+                for d in range(1, SHARE):
+                    share_copy(f, part, d).start()
+
+    def wait_inputs(part):
+        for f in range(2):
+            chip_copy(f, part).wait_recv()
+
+        @pl.when(outside)
+        def _():
+            for f in range(2):
+                for d in range(1, SHARE):
+                    share_copy(f, part, d).wait_recv()
+
+    def wait_inputs_sent():
+        for part in range(2):
+            for f in range(2):
+                chip_copy(f, part).wait_send()
+
+        @pl.when(outside)
+        def _():
+            for part in range(2):
+                for f in range(2):
+                    far_copy(f, part).wait_send()
+                    for d in range(1, SHARE):
+                        share_copy(f, part, d).wait_send()
 
     loads[1].wait()
     loads[2].wait()
-    send_halo((1, 2), 0)
+    send_inputs(0)
+    loads[0].wait()
+
+    @pl.when(t < nt - 1)
+    def _():
+        for i in range(3):
+            shift(i).start()
+
+    send_inputs(1)
 
     edge_y = lax.broadcasted_iota(jnp.int32, (ny, nx), 0)
     edge_x = lax.broadcasted_iota(jnp.int32, (ny, nx), 1)
@@ -159,6 +248,7 @@
              + (edge_x == 0).astype(f32) + (edge_x == nx - 1).astype(f32))
     keep_y = (edge_y < ny - 1).astype(f32) * (2 * SC)
     keep_x = (edge_x < nx - 1).astype(f32) * (2 * SC)
+    keep_l = (edge_x > 0).astype(f32) * (2 * SC)
     outer = outer * (2 * SC)
 
     def plane_weights(lo, hi):
@@ -166,10 +256,11 @@
             c = C[k]
             WY[k] = keep_y * (c + pltpu.roll(c, ny - 1, 0))
             WX[k] = keep_x * (c + pltpu.roll(c, nx - 1, 1))
+            WL[k] = keep_l * (c + pltpu.roll(c, 1, 1))
             E[k] = SC + outer * c
             return carry
 
-        loop(lo, hi, body, 0, 2)
+        loop(lo, hi, body, 0, 6)
 
     def face_weights(lo, hi):
         def body(k, carry):
@@ -183,12 +274,12 @@
             v = src(k)
             above = WZ[k + 1] * (src(k + 1) - v)
             fy = WY[k] * (pltpu.roll(v, ny - 1, 0) - v)
-            fx = WX[k] * (pltpu.roll(v, nx - 1, 1) - v)
-            out = E[k] * v - ((above - below) + (fy - pltpu.roll(fy, 1, 0)) + (fx - pltpu.roll(fx, 1, 1)))
+            fx = WX[k] * (pltpu.roll(v, nx - 1, 1) - v) + WL[k] * (pltpu.roll(v, 1, 1) - v)
+            out = E[k] * v - ((above - below) + (fy - pltpu.roll(fy, 1, 0)) + fx)
             dst(k, out, v)
             return above
 
-        loop(lo, hi, body, WZ[lo] * (src(lo) - src(lo - 1)), 2)
+        loop(lo, hi, body, WZ[lo] * (src(lo) - src(lo - 1)), APPLY)
 
     def from_x(k):
         return X[k]
@@ -275,40 +366,53 @@
 
         loop(lo, hi, body, 0, 2)
 
-    def section(which):
-        lo, hi = lambda d: a - d, lambda d: b + d
-        apply(from_x, start_residual, lo(6), hi(6))
+    def both_sides(f, d0, d1):
+        f(a - d1, a - d0)
+        f(b + d0, b + d1)
+
+    def more_weights(d0, d1):
+        both_sides(plane_weights, d0, d1)
+        face_weights(a - d1, a - d0)
+        face_weights(b + d0 + 1, b + d1 + 1)
+
+    def residual(lo, hi):
+        apply(from_x, start_residual, lo, hi)
+
+    def powers(buf, d0, d1, last):
+        for j in range(1, last + 1):
+            both_sides(functools.partial(power, buf, j), d0 - j, d1 - j)
+
+    def section(which, before=None):
+        residual(a - 3, b + 3)
         for j in (1, 2, 3):
-            power(V, j, lo(6 - j), hi(6 - j))
+            power(V, j, a - 3 + j, b + 3 - j)
         r = to_row(first_pairs, first_places, dots(first_pairs, ("v0", "v1", "v2", "v3")))
         send_row(2 * which, r)
         if which == 0:
-            send_halo((1, 2, 0), 1)
+            send_halo(2)
+            wait_inputs(1)
+            wait_halo(1, False)
+            more_weights(3, 6)
+        else:
+            before()
+        both_sides(residual, 3, 6)
+        powers(V, 3, 6, 3)
         tile = total_tile(2 * which, r)
         y1 = gauss_jordan(tile, 3)
         coefs = [spread(y1, j) for j in range(3)]
-        next_residual(coefs, lo(3), hi(3))
+        next_residual(coefs, a - 3, b + 3)
         for j in (1, 2, 3):
-            power(W, j, lo(3 - j), hi(3 - j))
+            power(W, j, a - 3 + j, b + 3 - j)
         r = to_row(second_pairs, second_places,
                    dots(second_pairs, ("v0", "v1", "v2", "v3", "w0", "w1", "w2", "w3")))
         send_row(2 * which + 1, r)
         if which == 0:
-            wait_halo((1, 2, 0), 1, False)
-            plane_weights(a - 12, a - 6)
-            plane_weights(b + 6, b + 12)
-            face_weights(a - 12, a - 6)
-            face_weights(b + 7, b + 13)
-            apply(from_x, start_residual, lo(12), lo(6))
-            apply(from_x, start_residual, hi(6), hi(12))
-            for j in (1, 2, 3):
-                power(V, j, lo(12 - j), lo(6 - j))
-                power(V, j, hi(6 - j), hi(12 - j))
-            next_residual(coefs, lo(9), lo(3))
-            next_residual(coefs, hi(3), hi(9))
-            for j in (1, 2):
-                power(W, j, lo(9 - j), lo(3 - j))
-                power(W, j, hi(3 - j), hi(9 - j))
+            wait_halo(2, False)
+            more_weights(6, 12)
+            both_sides(residual, 6, 12)
+            powers(V, 6, 12, 3)
+            both_sides(functools.partial(next_residual, coefs), 3, 9)
+            powers(W, 3, 9, 2)
         rows = lax.broadcasted_iota(jnp.int32, (8, 128), 0)
         lanes = lax.broadcasted_iota(jnp.int32, (8, 128), 1)
         old = jnp.logical_and(jnp.logical_and(rows < 3, lanes < 3), rows >= 0)
@@ -327,20 +431,28 @@
 
     loads[3].wait()
 
-    @pl.when(t > 0)
-    def _():
-        shift.wait_recv()
-
     def add(k, carry):
         X[a + k] = CP[k] + CR[k]
         return carry
 
-    loop(0, nz, add, 0, 4)
-    send_halo((0,), 0)
-
-    wait_halo((1, 2), 0, False)
-    plane_weights(a - 6, b + 6)
-    face_weights(a - 6, b + 7)
+    def arrive(i):
+        @pl.when(t > 0)
+        def _():
+            shift(i).wait_recv()
+
+        loop(pieces[i][0], sum(pieces[i]), add, 0, 4)
+
+    pass_inputs(0)
+    arrive(0)
+    arrive(1)
+    send_halo(0)
+    arrive(2)
+    send_halo(1)
+    pass_inputs(1)
+
+    wait_inputs(0)
+    plane_weights(a - 3, b + 3)
+    face_weights(a - 3, b + 4)
 
     @pl.when(jnp.logical_not(has_left))
     def _():
@@ -352,35 +464,36 @@
         WZ[b] = zero
         E[b - 1] = E[b - 1] + (2 * SC) * C[b - 1]
 
-    wait_halo((0,), 0, False)
+    wait_halo(0, False)
 
     result = section(0)
-    wait_halo((0,), 0, True)
-    wait_halo((0,), 1, True)
+    for level in range(3):
+        wait_halo(level, True)
 
     def put_x(k, carry):
-        X[k] = result(k)
+        X[k] = result0(k)
         return carry
 
-    loop(a - 7, b + 7, put_x, 0, 2)
+    result0 = result
+    loop(a - 4, b + 4, put_x, 0, 4)
     out0 = pltpu.make_async_copy(X.at[pl.ds(a, nz)], out_hbm.at[0], out_sem.at[0])
     out0.start()
-    result = section(1)
+    result = section(1, lambda: both_sides(lambda lo, hi: loop(lo, hi, put_x, 0, 3), 4, 7))
 
     def put_o(k, carry):
         O[k] = result(a + k)
         return carry
 
-    loop(0, nz, put_o, 0, 2)
+    loop(0, nz, put_o, 0, 4)
     out1 = pltpu.make_async_copy(O, out_hbm.at[1], out_sem.at[1])
     out1.start()
 
-    wait_halo((1, 2), 0, True)
-    wait_halo((1, 2), 1, True)
+    wait_inputs_sent()
 
     @pl.when(t < nt - 1)
     def _():
-        shift.wait_send()
+        for i in range(3):
+            shift(i).wait_send()
 
     out0.wait()
     out1.wait()
@@ -402,6 +515,7 @@
                 pltpu.VMEM((ext, ny, nx), f32),
                 pltpu.VMEM((ext, ny, nx), f32),
                 pltpu.VMEM((ext + 1, ny, nx), f32),
+                pltpu.VMEM((ext, ny, nx), f32),
                 pltpu.VMEM((ext, ny, nx), f32),
                 pltpu.VMEM((ext, ny, nx), f32),
                 pltpu.VMEM((ext, ny, nx), f32),
@@ -415,10 +529,16 @@
                 pltpu.VMEM((4, ns, 1, 128), f32),
                 pltpu.SemaphoreType.DMA((4,)),
                 pltpu.SemaphoreType.DMA((2,)),
-                pltpu.SemaphoreType.DMA((12,)),
-                pltpu.SemaphoreType.DMA((12,)),
-                pltpu.SemaphoreType.DMA,
-                pltpu.SemaphoreType.DMA,
+                pltpu.SemaphoreType.DMA((6,)),
+                pltpu.SemaphoreType.DMA((6,)),
+                pltpu.SemaphoreType.DMA((4,)),
+                pltpu.SemaphoreType.DMA((4,)),
+                pltpu.SemaphoreType.DMA((4,)),
+                pltpu.SemaphoreType.DMA((4,)),
+                pltpu.SemaphoreType.DMA((4 * (SHARE - 1),)),
+                pltpu.SemaphoreType.DMA((4 * (SHARE - 1),)),
+                pltpu.SemaphoreType.DMA((3,)),
+                pltpu.SemaphoreType.DMA((3,)),
                 pltpu.SemaphoreType.DMA((4, ns - 1)),
                 pltpu.SemaphoreType.DMA((4, ns - 1)),
             ],

time: 94 us -> 64 us (0.68)
  the two profiles are of different devices: /device:TPU:88 before, /device:TPU:248 now
where the time goes in v3:
time: 64 us; the launch traced here: 63.9 us
  Pallas kernels  62 us (97%)
  local copies, waits for them, and re-layouts  1.87 us (3%)
    pallas_call x1, Pallas kernels, body(): pl.pallas_call(functools.partial(kernel, ns, nt, nz), out_shape=jax.Shape...  62 us
    unnamed x1, local copies, waits for them, and re-layouts  1.87 us

profile of v3, /device:TPU:248, one launch (start us, length us, event | category | flops | bytes accessed | tf_op | source)
XLA Modules:
  0.0 63.9 jit_solution(7552219794522250001)
XLA Ops:
  0.0 62.0 %shard_map.46 = f32[2,16,32,128]{3,2,1,0:T(8,128)} custom-call(f32[16,32,128]{2,1,0:T(8,128)} %bitcast.4, f32[16,32,128]{2,1,0:T(8,128)} %bitcast.5, f32[16,32,128]{2,1,0:T(8,128)} %cond_hbm.1, f32[16,32,128]{2,1,0:T(8,128)} %force_hbm.1), custom_call_target="tpu_custom_call" | custom-call | tf_op jit(solution)/shard_map/pallas_call | solution.py:508
  62.0 1.9 %copy.6 = f32[1,2,16,32,128]{4,3,2,1,0:T(8,128)} copy(f32[1,2,16,32,128]{4,3,2,1,0:T(8,128)} %bitcast.3) | data formatting | bytes 1048576

commit v4 on v3

--- a/solution.py
+++ b/solution.py
@@ -29,19 +29,41 @@
     return lax.fori_loop(hi - rest, hi, body, init, unroll=rest) if rest else init
 
 
-def gauss_jordan(m, n):
-    rows = lax.broadcasted_iota(jnp.int32, (8, 128), 0)
-    first = m
-    for k in range(n):
-        row = jnp.broadcast_to(m[k : k + 1, :], (8, 128))
-        col = jnp.broadcast_to(m[:, k : k + 1], (8, 128))
-        pivot = jnp.broadcast_to(row[:, k : k + 1], (8, 128))
-        size = jnp.broadcast_to(jnp.broadcast_to(first[k : k + 1, :], (8, 128))[:, k : k + 1], (8, 128))
-        good = pivot > TOL * size
-        inverse = jnp.where(good, 1.0 / jnp.where(good, pivot, 1.0), 0.0)
-        row = row * inverse
-        m = jnp.where(rows == k, row, m - col * row)
-    return jnp.broadcast_to(m[:, 6:7], (8, 128))
+class Solver:
+    def __init__(self):
+        self.inverse, self.column, self.factor = [], [], []
+
+    def grow(self, rows):
+        for row in rows:
+            i = len(self.inverse)
+            row = list(row)
+            size = row[i]
+            factors = []
+            for k in range(i):
+                f = row[k] * self.inverse[k]
+                factors.append(f)
+                for j in range(k + 1, i):
+                    row[j] = row[j] - f * self.column[k][j - k - 1]
+                row[i] = row[i] - f * row[k]
+            for k in range(i):
+                self.column[k].append(row[k])
+                self.factor[k].append(factors[k])
+            good = row[i] > TOL * size
+            self.inverse.append(jnp.where(good, 1.0 / jnp.where(good, row[i], 1.0), 0.0))
+            self.column.append([])
+            self.factor.append([])
+
+    def solve(self, g):
+        g, n = list(g), len(g)
+        for k in range(n):
+            for i in range(k + 1, n):
+                g[i] = g[i] - self.factor[k][i - k - 1] * g[k]
+        y = [None] * n
+        for k in reversed(range(n)):
+            y[k] = g[k] * self.inverse[k]
+            for i in range(k + 1, n):
+                y[k] = y[k] - self.factor[k][i - k - 1] * y[i]
+        return y
 
 
 def kernel(ns, nt, nz, cp_hbm, co_hbm, cond_hbm, force_hbm, out_hbm, X, C, F, WZ, WY, WX, WL, E, V, W, CP, CO, CR, O,
@@ -306,22 +328,22 @@
 
     lane = lax.broadcasted_iota(jnp.int32, (1, 128), 1)
 
-    def to_row(pairs, places, accs):
+    def to_row(accs):
         r = jnp.zeros((1, 128), f32)
-        for pair, acc in zip(pairs, accs):
+        for n, acc in enumerate(accs):
             total = jnp.sum(jnp.sum(acc, axis=0, keepdims=True), axis=1, keepdims=True)
-            mask = None
-            for i, j in places[pair]:
-                m = lane == (j - 8 * i) % 128
-                mask = m if mask is None else jnp.logical_or(mask, m)
-            r = jnp.where(mask, jnp.broadcast_to(total, (1, 128)), r)
+            r = jnp.where(lane == n, jnp.broadcast_to(total, (1, 128)), r)
         return r
 
     def exchange(n, d):
         return pltpu.make_async_remote_copy(
-            row_buf.at[n], gather.at[n, s], ar_send.at[n, d - 1], ar_recv.at[n, d - 1],
+            row_buf.at[n], gather.at[n, s], ar_send.at[n], ar_recv.at[n],
             device_id={"space": lax.rem(s + d, ns)}, device_id_type=MESH,
         )
+
+    def all_rows(n, sem):
+        p = gather.at[n, pl.ds(0, ns - 1)]
+        return pltpu.make_async_copy(p, p, sem.at[n])
 
     order = sorted(range(1, ns), key=lambda d: -min(d, ns - d))
 
@@ -330,34 +352,30 @@
         for d in order:
             exchange(n, d).start()
 
-    def total_tile(n, r):
-        for d in order:
-            exchange(n, d).wait()
+    def totals(n, r, pairs):
+        all_rows(n, ar_recv).wait()
         parts = [jnp.where(s == q, r, gather[n, q]) for q in range(ns)]
         while len(parts) > 1:
             parts = [parts[i] + parts[i + 1] for i in range(0, len(parts), 2)]
-        return pltpu.roll(jnp.broadcast_to(parts[0], (8, 128)), 0, 1, stride=8, stride_axis=0)
-
-    first_pairs = (("v0", "v0"), ("v0", "v1"), ("v0", "v2"), ("v1", "v1"), ("v1", "v2"), ("v2", "v2"), ("v2", "v3"))
-    first_places = {
-        ("v0", "v0"): ((0, 6),), ("v0", "v1"): ((0, 0), (1, 6)), ("v0", "v2"): ((2, 6),),
-        ("v1", "v1"): ((1, 0), (0, 1)), ("v1", "v2"): ((1, 1), (2, 0), (0, 2)),
-        ("v2", "v2"): ((2, 1), (1, 2)), ("v2", "v3"): ((2, 2),),
-    }
-    second_pairs = [("w0", "v0")] + [(f"w{i}", f"v{j}") for i in range(3) for j in (1, 2, 3)]
-    second_places = {("w0", "v0"): ((0, 6),)}
-    for i in range(3):
-        for j in range(3):
-            second_places[(f"w{i}", f"v{j + 1}")] = ((3 + i, j), (j, 3 + i))
-    second_places[("w0", "v1")] += ((1, 6),)
-    second_places[("w0", "v2")] += ((2, 6),)
-    for pair, where in first_places.items():
-        q = tuple(p.replace("v", "w") for p in pair)
-        second_pairs.append(q)
-        second_places[q] = tuple((i + 3, j if j == 6 else j + 3) for i, j in where)
-
-    def spread(y, j):
-        return jnp.broadcast_to(y[j : j + 1, :], (ny, nx))
+        total = jnp.broadcast_to(parts[0], (8, 128))
+        return {p: jnp.broadcast_to(total[:, i : i + 1], (8, 128)) for i, p in enumerate(pairs)}
+
+    def own_pairs(u):
+        return [(u + "0", u + "0"), (u + "0", u + "1"), (u + "0", u + "2"), (u + "1", u + "1"), (u + "1", u + "2"),
+                (u + "2", u + "2"), (u + "2", u + "3")]
+
+    def own_rows(m, u):
+        return [[m[u + "0", u + "1"]], [m[u + "1", u + "1"], m[u + "1", u + "2"]],
+                [m[u + "1", u + "2"], m[u + "2", u + "2"], m[u + "2", u + "3"]]]
+
+    def own_side(m, u):
+        return [m[u + "0", u + "0"], m[u + "0", u + "1"], m[u + "0", u + "2"]]
+
+    first_pairs = own_pairs("v")
+    second_pairs = [("w0", "v0")] + [(f"w{i}", f"v{j}") for i in range(3) for j in (1, 2, 3)] + own_pairs("w")
+
+    def spread(y):
+        return jnp.concatenate([y] * (ny // 8), axis=0)
 
     def next_residual(coefs, lo, hi):
         def body(k, carry):
@@ -386,7 +404,7 @@
         residual(a - 3, b + 3)
         for j in (1, 2, 3):
             power(V, j, a - 3 + j, b + 3 - j)
-        r = to_row(first_pairs, first_places, dots(first_pairs, ("v0", "v1", "v2", "v3")))
+        r = to_row(dots(first_pairs, ("v0", "v1", "v2", "v3")))
         send_row(2 * which, r)
         if which == 0:
             send_halo(2)
@@ -397,14 +415,15 @@
             before()
         both_sides(residual, 3, 6)
         powers(V, 3, 6, 3)
-        tile = total_tile(2 * which, r)
-        y1 = gauss_jordan(tile, 3)
-        coefs = [spread(y1, j) for j in range(3)]
+        m = totals(2 * which, r, first_pairs)
+        solver = Solver()
+        solver.grow(own_rows(m, "v"))
+        y1 = solver.solve(own_side(m, "v"))
+        coefs = [spread(y) for y in y1]
         next_residual(coefs, a - 3, b + 3)
         for j in (1, 2, 3):
             power(W, j, a - 3 + j, b + 3 - j)
-        r = to_row(second_pairs, second_places,
-                   dots(second_pairs, ("v0", "v1", "v2", "v3", "w0", "w1", "w2", "w3")))
+        r = to_row(dots(second_pairs, ("v0", "v1", "v2", "v3", "w0", "w1", "w2", "w3")))
         send_row(2 * which + 1, r)
         if which == 0:
             wait_halo(2, False)
@@ -413,14 +432,11 @@
             powers(V, 6, 12, 3)
             both_sides(functools.partial(next_residual, coefs), 3, 9)
             powers(W, 3, 9, 2)
-        rows = lax.broadcasted_iota(jnp.int32, (8, 128), 0)
-        lanes = lax.broadcasted_iota(jnp.int32, (8, 128), 1)
-        old = jnp.logical_and(jnp.logical_and(rows < 3, lanes < 3), rows >= 0)
-        tile2 = jnp.where(old, tile, total_tile(2 * which + 1, r))
-        y2 = gauss_jordan(tile2, 6)
-        both = [(y1 + y2) * SC, y2 * SC]
-        cv = [spread(both[0], j) for j in range(3)]
-        cw = [spread(both[1], 3 + j) for j in range(3)]
+        m = totals(2 * which + 1, r, second_pairs)
+        solver.grow([[m[f"w{i}", f"v{j}"] for j in (1, 2, 3)] + row for i, row in enumerate(own_rows(m, "w"))])
+        y2 = solver.solve([m["w0", "v0"], m["w0", "v1"], m["w0", "v2"]] + own_side(m, "w"))
+        cv = [spread((y1[j] + y2[j]) * SC) for j in range(3)]
+        cw = [spread(y2[3 + j] * SC) for j in range(3)]
 
         def result(k):
             v = (cv[0] * V[0, k] + cv[1] * V[1, k]) + cv[2] * V[2, k]
@@ -489,6 +505,8 @@
     out1.start()
 
     wait_inputs_sent()
+    for n in range(4):
+        all_rows(n, ar_send).wait()
 
     @pl.when(t < nt - 1)
     def _():
@@ -539,8 +557,8 @@
                 pltpu.SemaphoreType.DMA((4 * (SHARE - 1),)),
                 pltpu.SemaphoreType.DMA((3,)),
                 pltpu.SemaphoreType.DMA((3,)),
-                pltpu.SemaphoreType.DMA((4, ns - 1)),
-                pltpu.SemaphoreType.DMA((4, ns - 1)),
+                pltpu.SemaphoreType.DMA((4,)),
+                pltpu.SemaphoreType.DMA((4,)),
             ],
             compiler_params=pltpu.CompilerParams(collective_id=0, has_side_effects=True),
         )(c_points[0], corrections[0], conductivity, forcing)

time: 64 us -> 61 us (0.953)
  Pallas kernels: 62 us -> 58.9 us
    pallas_call x1, Pallas kernels: 62 us -> 58.9 us  [body(): pl.pallas_call(functools.partial(kernel, ns, nt, nz), out_shape=jax.Shape...]
where the time goes in v4:
time: 61 us; the launch traced here: 60.8 us
  Pallas kernels  58.9 us (97%)
  local copies, waits for them, and re-layouts  1.87 us (3%)
    pallas_call x1, Pallas kernels, body(): pl.pallas_call(functools.partial(kernel, ns, nt, nz), out_shape=jax.Shape...  58.9 us
    unnamed x1, local copies, waits for them, and re-layouts  1.87 us

profile of v4, /device:TPU:248, one launch (start us, length us, event | category | flops | bytes accessed | tf_op | source)
XLA Modules:
  0.0 60.8 jit_solution(4482598579152518121)
XLA Ops:
  0.0 58.9 %shard_map.46 = f32[2,16,32,128]{3,2,1,0:T(8,128)} custom-call(f32[16,32,128]{2,1,0:T(8,128)} %bitcast.4, f32[16,32,128]{2,1,0:T(8,128)} %bitcast.5, f32[16,32,128]{2,1,0:T(8,128)} %cond_hbm.1, f32[16,32,128]{2,1,0:T(8,128)} %force_hbm.1), custom_call_target="tpu_custom_call" | custom-call | tf_op jit(solution)/shard_map/pallas_call | solution.py:526
  58.9 1.9 %copy.6 = f32[1,2,16,32,128]{4,3,2,1,0:T(8,128)} copy(f32[1,2,16,32,128]{4,3,2,1,0:T(8,128)} %bitcast.3) | data formatting | bytes 1048576

commit v5 on v4

--- a/solution.py
+++ b/solution.py
@@ -324,7 +324,7 @@
                 out.append(acc + ((z[0:8] + z[8:16]) + (z[16:24] + z[24:32])))
             return tuple(out)
 
-        return loop(a, b, body, tuple(jnp.zeros((8, nx), f32) for _ in pairs), 2)
+        return loop(a, b, body, tuple(jnp.zeros((8, nx), f32) for _ in pairs), 16)
 
     lane = lax.broadcasted_iota(jnp.int32, (1, 128), 1)
 
@@ -382,7 +382,7 @@
             W[0, k] = V[0, k] - (coefs[0] * V[1, k] + coefs[1] * V[2, k] + coefs[2] * V[3, k])
             return carry
 
-        loop(lo, hi, body, 0, 2)
+        loop(lo, hi, body, 0, 8)
 
     def both_sides(f, d0, d1):
         f(a - d1, a - d0)
@@ -458,10 +458,10 @@
 
         loop(pieces[i][0], sum(pieces[i]), add, 0, 4)
 
-    pass_inputs(0)
     arrive(0)
     arrive(1)
     send_halo(0)
+    pass_inputs(0)
     arrive(2)
     send_halo(1)
     pass_inputs(1)
@@ -500,7 +500,7 @@
         O[k] = result(a + k)
         return carry
 
-    loop(0, nz, put_o, 0, 4)
+    loop(0, nz, put_o, 0, 8)
     out1 = pltpu.make_async_copy(O, out_hbm.at[1], out_sem.at[1])
     out1.start()
 

time: 61 us -> 59.5 us (0.975)
  the two profiles are of different devices: /device:TPU:248 before, /device:TPU:1 now
where the time goes in v5:
time: 59.5 us; the launch traced here: 59.4 us
  Pallas kernels  57.5 us (97%)
  local copies, waits for them, and re-layouts  1.87 us (3%)
    pallas_call x1, Pallas kernels, body(): pl.pallas_call(functools.partial(kernel, ns, nt, nz), out_shape=jax.Shape...  57.5 us
    unnamed x1, local copies, waits for them, and re-layouts  1.87 us

profile of v5, /device:TPU:1, one launch (start us, length us, event | category | flops | bytes accessed | tf_op | source)
XLA Modules:
  0.0 59.4 jit_solution(13411256037957324712)
XLA Ops:
  0.0 57.5 %shard_map.46 = f32[2,16,32,128]{3,2,1,0:T(8,128)} custom-call(f32[16,32,128]{2,1,0:T(8,128)} %bitcast.4, f32[16,32,128]{2,1,0:T(8,128)} %bitcast.5, f32[16,32,128]{2,1,0:T(8,128)} %cond_hbm.1, f32[16,32,128]{2,1,0:T(8,128)} %force_hbm.1), custom_call_target="tpu_custom_call" | custom-call | tf_op jit(solution)/shard_map/pallas_call | solution.py:526
  57.5 1.9 %copy.6 = f32[1,2,16,32,128]{4,3,2,1,0:T(8,128)} copy(f32[1,2,16,32,128]{4,3,2,1,0:T(8,128)} %bitcast.3) | data formatting | bytes 1048576

commit v6 on v5

--- a/solution.py
+++ b/solution.py
@@ -401,9 +401,16 @@
             both_sides(functools.partial(power, buf, j), d0 - j, d1 - j)
 
     def section(which, before=None):
-        residual(a - 3, b + 3)
-        for j in (1, 2, 3):
-            power(V, j, a - 3 + j, b + 3 - j)
+        if which == 0:
+            residual(a - 3, a + 1)
+            residual(b - 1, b + 3)
+            for j in (1, 2, 3):
+                power(V, j, a - 3 + j, a + 1 + j)
+                power(V, j, b - 1 - j, b + 3 - j)
+        else:
+            residual(a - 3, b + 3)
+            for j in (1, 2, 3):
+                power(V, j, a - 3 + j, b + 3 - j)
         r = to_row(dots(first_pairs, ("v0", "v1", "v2", "v3")))
         send_row(2 * which, r)
         if which == 0:
@@ -458,17 +465,23 @@
 
         loop(pieces[i][0], sum(pieces[i]), add, 0, 4)
 
+    plane_weights(a, b)
+    face_weights(a + 1, b)
     arrive(0)
     arrive(1)
     send_halo(0)
     pass_inputs(0)
     arrive(2)
     send_halo(1)
+    residual(a + 1, b - 1)
+    for j in (1, 2, 3):
+        power(V, j, a + 1 + j, b - 1 - j)
     pass_inputs(1)
 
     wait_inputs(0)
-    plane_weights(a - 3, b + 3)
-    face_weights(a - 3, b + 4)
+    both_sides(plane_weights, 0, 3)
+    face_weights(a - 3, a + 1)
+    face_weights(b, b + 4)
 
     @pl.when(jnp.logical_not(has_left))
     def _():

time: 59.5 us -> 59.5 us (level)
  no operation moved by 1% of the time
where the time goes in v6:
time: 59.5 us; the launch traced here: 59.4 us
  Pallas kernels  57.5 us (97%)
  local copies, waits for them, and re-layouts  1.87 us (3%)
    pallas_call x1, Pallas kernels, body(): pl.pallas_call(functools.partial(kernel, ns, nt, nz), out_shape=jax.Shape...  57.5 us
    unnamed x1, local copies, waits for them, and re-layouts  1.87 us

profile of v6, /device:TPU:1, one launch (start us, length us, event | category | flops | bytes accessed | tf_op | source)
XLA Modules:
  0.0 59.4 jit_solution(5495398276802915727)
XLA Ops:
  0.0 57.5 %shard_map.46 = f32[2,16,32,128]{3,2,1,0:T(8,128)} custom-call(f32[16,32,128]{2,1,0:T(8,128)} %bitcast.4, f32[16,32,128]{2,1,0:T(8,128)} %bitcast.5, f32[16,32,128]{2,1,0:T(8,128)} %cond_hbm.1, f32[16,32,128]{2,1,0:T(8,128)} %force_hbm.1), custom_call_target="tpu_custom_call" | custom-call | tf_op jit(solution)/shard_map/pallas_call | solution.py:539
  57.5 1.9 %copy.6 = f32[1,2,16,32,128]{4,3,2,1,0:T(8,128)} copy(f32[1,2,16,32,128]{4,3,2,1,0:T(8,128)} %bitcast.3) | data formatting | bytes 1048576
